TPU v7x, 32 devices: a whole 2x2x4 slice. The times are simulated.
32 devices in a mesh: chan: 4 (over z), pulse: 4 (over x, core), range: 2 (over y).
Axes of the slice: x: 2, y: 2, z: 4, core: 2. Of those that a mesh axis runs over, the one named last changes fastest.
Arguments:
- signal: bfloat16 [2, 64, 32, 8192], P(None, 'chan', 'pulse', 'range'), may hold values from -6 to 6
- steering: bfloat16 [2, 32, 64], replicated, may hold values from -0.5 to 0.5
- spectrum: float32 [2, 8192], replicated, may hold values from -6 to 6
Outputs:
- detection: float32 [32, 32, 8192], P('chan', 'pulse', 'range')
All inputs are finite; a program needn't handle non-finite values.
Results may differ from a plain program's by a relative error of at most 0.0087.
Values may be sent and summed in bfloat16 or wider, within the bound.
A program may use at most 64 MiB of HBM per device.

v0:
```python
import math

import jax
import jax.numpy as jnp
from jax import lax
from jax.sharding import PartitionSpec as P

GUARD = 4
TRAIN = 16


PRECISE = lax.Precision.HIGHEST
NOISE_FLOOR = 0.25


def padded_2(x, sides, width):
    for axis, dim in sides:
        peers, length = (lax.axis_size(axis), x.shape[dim])
        up = [(i, (i + 1) % peers) for i in range(peers - 1)]
        down = [(j, i) for i, j in up]
        last = lax.slice_in_dim(x, length - width, length, axis=dim)
        initial = lax.slice_in_dim(x, 0, width, axis=dim)
        before = lax.ppermute(last, axis, up)
        after = lax.ppermute(initial, axis, down)
        x = jnp.concatenate([before, x, after], axis=dim)
    return x


def doppler_tables(pulse_count):
    row_ids = lax.broadcasted_iota(jnp.int32, (pulse_count, pulse_count), 0)
    col_ids = lax.broadcasted_iota(jnp.int32, (pulse_count, pulse_count), 1)
    phase_angle = (row_ids * col_ids % pulse_count).astype(jnp.float32) * (
        2.0 * math.pi / pulse_count
    )
    norm_scale = 1.0 / math.sqrt(pulse_count)
    table_real = (jnp.cos(phase_angle) * norm_scale).astype(jnp.bfloat16)
    table_imag = (-jnp.sin(phase_angle) * norm_scale).astype(jnp.bfloat16)
    return (table_real, table_imag)


def phase_table(row_count, col_count, period_len, direction):
    row_ids = lax.broadcasted_iota(jnp.int32, (row_count, col_count), 0)
    col_ids = lax.broadcasted_iota(jnp.int32, (row_count, col_count), 1)
    phase_angle = (row_ids * col_ids % period_len).astype(jnp.float32) * (
        2.0 * math.pi / period_len
    )
    return (jnp.cos(phase_angle), direction * jnp.sin(phase_angle))


def rotate_by(field_pair, table_pair):
    return (
        field_pair[0] * table_pair[0] - field_pair[1] * table_pair[1],
        field_pair[0] * table_pair[1] + field_pair[1] * table_pair[0],
    )


def mix_blocks(table_pair, field_pair):

    def contract(table_part, field_part):
        return jnp.einsum("km,bpmn->bpkn", table_part, field_part, precision=PRECISE)

    return (
        contract(table_pair[0], field_pair[0]) - contract(table_pair[1], field_pair[1]),
        contract(table_pair[0], field_pair[1]) + contract(table_pair[1], field_pair[0]),
    )


def mix_lanes(field_pair, table_pair):

    def contract(field_part, table_part):
        return jnp.einsum("bpkm,mn->bpkn", field_part, table_part, precision=PRECISE)

    return (
        contract(field_pair[0], table_pair[0]) - contract(field_pair[1], table_pair[1]),
        contract(field_pair[0], table_pair[1]) + contract(field_pair[1], table_pair[0]),
    )


def local_transform(field_pair, direction):
    size_all = field_pair[0].shape[-1]
    blocks = size_all // 128
    leading = field_pair[0].shape[:-1]
    shaped = tuple((member.reshape(leading + (blocks, 128)) for member in field_pair))
    outer_table = phase_table(blocks, blocks, blocks, direction)
    twiddle = phase_table(blocks, 128, size_all, direction)
    inner_table = phase_table(128, 128, 128, direction)
    if direction < 0:
        shaped = mix_blocks(outer_table, shaped)
        shaped = rotate_by(shaped, twiddle)
        shaped = mix_lanes(shaped, inner_table)
    else:
        shaped = mix_lanes(shaped, inner_table)
        shaped = rotate_by(shaped, twiddle)
        shaped = mix_blocks(outer_table, shaped)
    return tuple((member.reshape(leading + (size_all,)) for member in shaped))


def stack_weights(w_real, w_imag):
    return jnp.concatenate(
        [jnp.concatenate([w_real, -w_imag], 1), jnp.concatenate([w_imag, w_real], 1)], 0
    )


def shards(signal, steering, spectrum):
    beam_count = steering.shape[1]
    chan_count = steering.shape[2]
    pulse_local = signal.shape[2]
    gate_count = signal.shape[3]
    stacked = stack_weights(steering[0], steering[1])
    samples = lax.all_to_all(signal, "chan", split_axis=2, concat_axis=1, tiled=True)
    pulses_here = samples.shape[2]
    gates_here = samples.shape[3]
    flat_samples = samples.reshape(2 * chan_count, pulses_here * gates_here)
    formed = jnp.dot(stacked, flat_samples, preferred_element_type=jnp.float32)
    formed = formed.astype(jnp.bfloat16).reshape(2, beam_count, pulses_here, gates_here)
    beam_data = lax.all_to_all(formed, "chan", split_axis=1, concat_axis=2, tiled=True)
    beam_local = beam_data.shape[1]
    range_count = lax.axis_size("range")
    range_index = lax.axis_index("range")
    full_length = gate_count * range_count
    inverse_scale = 1.0 / full_length
    shard_piece = lax.all_gather(beam_data, "range", axis=3, tiled=True)
    shard_count = shard_piece.shape[3] // gate_count
    members = shard_piece.astype(jnp.float32).reshape(
        2, beam_local, pulse_local, shard_count, gate_count
    )
    source = jnp.arange(shard_count, dtype=jnp.int32)
    phase_angle = (source * range_index % range_count).astype(jnp.float32) * (
        2.0 * math.pi / range_count
    )
    cos_part = jnp.cos(phase_angle)[:, None]
    sin_part = -jnp.sin(phase_angle)[:, None]
    sum_real = jnp.sum(members[0] * cos_part - members[1] * sin_part, axis=2)
    sum_imag = jnp.sum(members[0] * sin_part + members[1] * cos_part, axis=2)
    folded = (sum_real, sum_imag)
    gate_ids = lax.broadcasted_iota(jnp.int32, (gate_count,), 0)
    global_angle = (gate_ids * range_index % full_length).astype(jnp.float32) * (
        2.0 * math.pi / full_length
    )
    folded = rotate_by(folded, (jnp.cos(global_angle), -jnp.sin(global_angle)))
    spectrum_local = local_transform(folded, -1.0)
    response = spectrum.reshape(2, gate_count, range_count)
    response = lax.dynamic_index_in_dim(response, range_index, axis=2, keepdims=False)
    response = jnp.transpose(response.reshape(2, 128, gate_count // 128), (0, 2, 1)).reshape(
        2, gate_count
    )
    filtered = rotate_by(spectrum_local, (response[0], response[1]))
    restored = local_transform(filtered, 1.0)
    restored = rotate_by(restored, (jnp.cos(global_angle), jnp.sin(global_angle)))
    shard_piece = (
        lax.all_gather(restored[0], "range", axis=2, tiled=True),
        lax.all_gather(restored[1], "range", axis=2, tiled=True),
    )
    shard_count = shard_piece[0].shape[2] // gate_count
    rows_real = shard_piece[0].reshape(beam_local, pulse_local, shard_count, gate_count)
    rows_imag = shard_piece[1].reshape(beam_local, pulse_local, shard_count, gate_count)
    source = jnp.arange(shard_count, dtype=jnp.int32)
    phase_angle = (source * range_index % range_count).astype(jnp.float32) * (
        2.0 * math.pi / range_count
    )
    cos_part = jnp.cos(phase_angle)[:, None]
    sin_part = jnp.sin(phase_angle)[:, None]
    sum_real = jnp.sum(rows_real * cos_part - rows_imag * sin_part, axis=2)
    sum_imag = jnp.sum(rows_real * sin_part + rows_imag * cos_part, axis=2)
    compressed = jnp.stack([sum_real * inverse_scale, sum_imag * inverse_scale]).astype(
        jnp.bfloat16
    )
    pulse_total = pulse_local * lax.axis_size("pulse")
    dop_real, dop_imag = doppler_tables(pulse_total)
    columns = lax.all_to_all(compressed, "pulse", split_axis=3, concat_axis=2, tiled=True)

    def product(table_part, values):
        return jnp.einsum("fp,bpr->bfr", table_part, values, preferred_element_type=jnp.float32)

    mixed_real = product(dop_real, columns[0]) - product(dop_imag, columns[1])
    mixed_imag = product(dop_real, columns[1]) + product(dop_imag, columns[0])
    power_part = lax.all_to_all(
        mixed_real * mixed_real + mixed_imag * mixed_imag,
        "pulse",
        split_axis=1,
        concat_axis=2,
        tiled=True,
    )
    halo_width = GUARD + TRAIN
    padded = padded_2(power_part, (("range", 2),), halo_width)
    window_sum = jnp.zeros_like(power_part)
    for offset in range(1, TRAIN + 1):
        left_start = halo_width - GUARD - offset
        right_start = halo_width + GUARD + offset
        window_sum = (
            window_sum
            + padded[:, :, left_start : left_start + gate_count]
            + padded[:, :, right_start : right_start + gate_count]
        )
    noise_level = window_sum / (2.0 * TRAIN)
    return power_part / (noise_level + NOISE_FLOOR)


def solution(mesh):
    in_specs = (P(None, "chan", "pulse", "range"), P(), P())
    out_specs = P("chan", "pulse", "range")
    return jax.shard_map(shards, mesh=mesh, in_specs=in_specs, out_specs=out_specs, check_vma=False)
```

profile of v0, /device:TPU:0, one launch (start us, length us, event | category | flops | bytes accessed | tf_op | source)
XLA Modules:
  0.0 388.4 jit_solution(4963313028370823325)
XLA Ops:
  6.5 4.1 %copy.81 = bf16[2,16,8,4096]{3,1,0,2:T(8,128)(2,1)} copy(bf16[2,16,8,4096]{3,2,1,0:T(8,128)(2,1)} %param.3) | data formatting | bytes 4194304 | tf_op args[0]
  10.6 6.5 %all-to-all-start = ((bf16[2,16,8,4096]{3,1,0,2:T(8,128)(2,1)}), bf16[2,16,8,4096]{3,1,0,2:T(8,128)(2,1)S(1)}, u32[]{:S(2)}, u32[]{:S(2)}) async-start(bf16[2,16,8,4096]{3,1,0,2:T(8,128)(2,1)} %copy.81), calls=%async_computation | async-start | bytes 4194304 | tf_op jit(solution)/shard_map/all_to_all | solution.py:110
  17.1 48.2 %all-to-all-done = bf16[2,16,8,4096]{3,1,0,2:T(8,128)(2,1)S(1)} async-done(((bf16[2,16,8,4096]{3,1,0,2:T(8,128)(2,1)}), bf16[2,16,8,4096]{3,1,0,2:T(8,128)(2,1)S(1)}, u32[]{:S(2)}, u32[]{:S(2)}) %all-to-all-start) | async-done | bytes 2097184 | tf_op jit(solution)/shard_map/all_to_all | solution.py:110
  65.3 2.2 copy.82
  71.0 27.7 %all_to_all.66 = bf16[2,32,2,4096]{3,2,0,1:T(2,128)(2,1)S(1)} all-to-all(bf16[2,32,2,4096]{3,2,0,1:T(2,128)(2,1)S(1)} %copy.83), channel_id=1, replica_groups=mesh['chan'=4,'pulse'=4,'range'=2] {'chan'}, dimensions={1} | all-to-all | bytes 2097152 | tf_op jit(solution)/shard_map/all_to_all | solution.py:116
  100.6 6.4 %reshape.188 = f32[2,4096,2]{2,1,0:T(8,128)} reshape(f32[2,8192]{1,0:T(2,128)S(1)} %copy-done.1) | data formatting | bytes 131072 | tf_op jit(solution)/shard_map/reshape | solution.py:142
  107.0 4.7 %dynamic-slice_reduce_fusion = f32[2,4096]{1,0:T(2,128)S(1)} fusion(f32[2,4096,2]{2,1,0:T(8,128)} %reshape.188, s32[]{:T(128)S(6)} %select_n.134), kind=kLoop, calls=%fused_computation.31 | loop fusion | bytes 65540 | tf_op jit(solution)/shard_map/jit(dynamic_index_in_dim)/dynamic_slice | solution.py:143
  112.5 20.2 %all-gather.4.cloned.1.call-done = bf16[2,8,8,8192]{3,1,2,0:T(8,128)(2,1)} async-done(((bf16[2,8,8,4096]{3,1,2,0:T(8,128)(2,1)}), bf16[2,8,8,8192]{3,1,2,0:T(8,128)(2,1)}) %all-gather.4.cloned.1.call-update) | async-done | bytes 2097168 | tf_op jit(solution)/shard_map/all_gather | solution.py:122
  132.7 3.9 %fusion.271 = (f32[1,8,8,8192]{3,1,2,0:T(8,128)}, f32[1,8,8,8192]{3,1,2,0:T(8,128)}) fusion(bf16[2,8,8,8192]{3,1,2,0:T(8,128)(2,1)} %all-gather.4.cloned.1.call-done), kind=kLoop, calls=%fused_computation.365 | loop fusion | bytes 8388608 | tf_op jit(solution)/shard_map/slice | solution.py:133
  136.6 3.0 reshape.202
  139.7 4.4 %reshape.203 = f32[8,8,2,4096]{3,2,0,1:T(2,128)} reshape(f32[1,8,8,8192]{3,1,2,0:T(8,128)} %get-tuple-element.12) | data formatting | bytes 4194304 | tf_op jit(solution)/shard_map/squeeze | solution.py:133
  144.1 5.8 %subtract_reduce_fusion.1 = (f32[8,8,4096]{2,1,0:T(8,128)S(1)}, f32[8,8,4096]{2,1,0:T(8,128)S(1)}) fusion(f32[8,8,2,4096]{3,2,0,1:T(2,128)} %reshape.203, f32[8,8,2,4096]{3,2,0,1:T(2,128)S(1)} %reshape.202, f32[2]{0:T(128)S(1)} %get-tuple-element.24, f32[2]{0:T(128)S(1)} %get-tuple-element.23), kind=kLoop, calls=%fused_computation.35 | loop fusion | flops 3670016 | bytes 6291472 | tf_op jit(solution)/shard_map/reduce_sum | solution.py:133
  152.6 1.5 fusion.84
  154.1 1.5 fusion.2
  155.6 1.5 fusion.3
  169.8 2.2 fusion
  172.0 2.4 reshape.191
  174.3 2.2 fusion.1
  176.5 1.5 reshape.190
  178.1 1.6 multiply_subtract_fusion
  180.4 32.5 %all-gather.6.cloned.1.call-done = f32[8,8,8192]{2,1,0:T(8,128)} async-done(((f32[8,8,4096]{2,1,0:T(8,128)}), f32[8,8,8192]{2,1,0:T(8,128)}) %all-gather.6.cloned.1.call-update) | async-done | bytes 2097168 | tf_op jit(solution)/shard_map/all_gather | solution.py:151
  212.9 34.7 %all-gather.8.cloned.1.call-done = f32[8,8,8192]{2,1,0:T(8,128)} async-done(((f32[8,8,4096]{2,1,0:T(8,128)}), f32[8,8,8192]{2,1,0:T(8,128)}) %all-gather.8.cloned.1.call-update) | async-done | bytes 2097168 | tf_op jit(solution)/shard_map/all_gather | solution.py:152
  247.6 3.2 subtract_reduce_fusion
  252.1 14.0 %copy.106 = bf16[2,8,8,4096]{2,1,0,3:T(8,128)(2,1)} copy(bf16[2,8,8,4096]{3,1,2,0:T(8,128)(2,1)S(1)} %pad_maximum_fusion.2) | data formatting | bytes 2097152 | tf_op jit(solution)/shard_map/stack | solution.py:165
  266.1 20.5 %reshape.205 = bf16[4,2,65536]{2,1,0:T(2,128)(2,1)S(1)} reshape(bf16[4096,2,8,8]{3,2,1,0:T(8,128)(2,1)} %bitcast.133) | data formatting | bytes 2097152
  286.6 17.2 %all_to_all.67 = bf16[4,2,65536]{2,1,0:T(2,128)(2,1)S(1)} all-to-all(bf16[4,2,65536]{2,1,0:T(2,128)(2,1)S(1)} %reshape.205), channel_id=1, replica_groups=mesh['chan'=4,'pulse'=4,'range'=2] {'pulse'}, dimensions={0} | all-to-all | bytes 2097152 | tf_op jit(solution)/shard_map/all_to_all | solution.py:170
  303.8 21.7 %reshape.206 = bf16[4096,2,8,8]{3,2,1,0:T(8,128)(2,1)} reshape(bf16[4,2,65536]{2,1,0:T(2,128)(2,1)S(1)} %all_to_all.67) | data formatting | bytes 2097152
  325.5 16.0 %copy.107 = bf16[2,8,8,4,1024]{4,2,3,1,0:T(8,128)(2,1)S(1)} copy(bf16[2,8,8,4,1024]{2,1,0,4,3:T(8,128)(2,1)} %bitcast.134) | data formatting | bytes 2097152 | tf_op jit(solution)/shard_map/all_to_all | solution.py:170
  343.6 16.9 %all_to_all.68 = f32[8,32,1024]{2,0,1:T(8,128)S(1)} all-to-all(f32[8,32,1024]{2,0,1:T(8,128)S(1)} %copy.108), channel_id=1, replica_groups=mesh['chan'=4,'pulse'=4,'range'=2] {'pulse'}, dimensions={1} | all-to-all | bytes 2097152 | tf_op jit(solution)/shard_map/all_to_all | solution.py:177
  361.2 2.4 collective-permute-start
  365.2 4.2 %collective-permute-done.1 = f32[8,8,20]{2,1,0:T(8,128)S(1)} collective-permute-done((f32[8,8,20]{2,1,0:T(8,128)S(1)}, f32[8,8,20]{2,1,0:T(8,128)S(1)}, u32[]{:S(2)}, u32[]{:S(2)}) %collective-permute-start.1) | collective-permute-done | bytes 5152 | tf_op jit(solution)/shard_map/ppermute | solution.py:24
  369.4 12.0 %fusion.14 = f32[8,8,4096]{2,1,0:T(8,128)} fusion(f32[8,8,4096]{2,1,0:T(8,128)S(1)} %bitcast.151, f32[8,8,20]{2,1,0:T(8,128)S(1)} %collective-permute-done.1, f32[8,8,20]{2,1,0:T(8,128)S(1)} %collective-permute-done), kind=kLoop, calls=%fused_computation.60 | loop fusion | flops 17301504 | bytes 2107392 | tf_op jit(solution)/shard_map/div | solution.py:196
  (55 shorter events, 27.8 us)
Async XLA Ops:
  10.6 6.5 %copy-start.2 = (bf16[2,32,64]{2,1,0:T(8,128)(2,1)S(1)}, bf16[2,32,64]{2,1,0:T(8,128)(2,1)}, u32[]{:S(2)}) copy-start(bf16[2,32,64]{2,1,0:T(8,128)(2,1)} %param.4) | copy-start | bytes 24580
  10.6 54.7 %all-to-all-start = ((bf16[2,16,8,4096]{3,1,0,2:T(8,128)(2,1)}), bf16[2,16,8,4096]{3,1,0,2:T(8,128)(2,1)S(1)}, u32[]{:S(2)}, u32[]{:S(2)}) async-start(bf16[2,16,8,4096]{3,1,0,2:T(8,128)(2,1)} %copy.81), calls=%async_computation | async-start | bytes 4194304 | tf_op jit(solution)/shard_map/all_to_all | solution.py:110
  17.1 115.6 %all-gather.4.cloned.1.call-start = ((), (), s32[]{:S(2)}) async-start(), calls=%async_computation.4 | async-start | bytes 3145728 | tf_op jit(solution)/shard_map/all_gather | solution.py:122
  99.3 1.3 copy-start.1
  100.4 112.5 %all-gather.6.cloned.1.call-start = ((), (), s32[]{:S(2)}) async-start(), calls=%async_computation.5 | async-start | bytes 3145728 | tf_op jit(solution)/shard_map/all_gather | solution.py:151
  176.5 1.5 copy-start
  179.7 67.9 %all-gather.8.cloned.1.call-start = ((), (), s32[]{:S(2)}) async-start(), calls=%async_computation.6 | async-start | bytes 3145728 | tf_op jit(solution)/shard_map/all_gather | solution.py:152
  361.2 4.0 %collective-permute-start = (f32[8,8,20]{2,1,0:T(8,128)S(1)}, f32[8,8,20]{2,1,0:T(8,128)S(1)}, u32[]{:S(2)}, u32[]{:S(2)}) collective-permute-start(f32[8,8,20]{2,1,0:T(8,128)S(1)} %get-tuple-element.13), channel_id=1, source_target_pairs={{0,1},{2,3},{4,5},{6,7},{8,9},{10,11},{12,13},{14,15},{16,17},{18,... | collective-permute-start | bytes 15368 | tf_op jit(solution)/shard_map/ppermute | solution.py:23
  363.6 5.8 %collective-permute-start.1 = (f32[8,8,20]{2,1,0:T(8,128)S(1)}, f32[8,8,20]{2,1,0:T(8,128)S(1)}, u32[]{:S(2)}, u32[]{:S(2)}) collective-permute-start(f32[8,8,20]{2,1,0:T(8,128)S(1)} %get-tuple-element.14), channel_id=1, source_target_pairs={{1,0},{3,2},{5,4},{7,6},{9,8},{11,10},{13,12},{15,14},{17,16},{19,... | collective-permute-start | bytes 15368 | tf_op jit(solution)/shard_map/ppermute | solution.py:24
Sparse Core Ops, SparseCore 0:
  100.5 32.1 all-gather.3
  179.8 33.0 all-gather.5
  214.5 33.0 all-gather.7
where the time goes:
time: 395 us; the launch traced here: 388 us
  waiting for transfers between devices  141 us (36%)
  local copies, waits for them, and re-layouts  112 us (28%)
  blocking collectives  61.8 us (16%)
  matrix products  24.9 us (6%)
  other arithmetic  24.3 us (6%)
  between operations  13.9 us (4%)
  starting transfers between devices  10.5 us (3%)
    unnamed x12, local copies, waits for them, and re-layouts  48.9 us
    all_to_all x1, waiting for transfers between devices, shards(): lax.all_to_all(signal, 'chan', split_axis=2, concat_axis=1, tiled=True)  48.2 us
    all_gather x1, waiting for transfers between devices, shards(): lax.all_gather(restored[1], 'range', axis=2, tiled=True)  34.7 us
    all_gather x1, waiting for transfers between devices, shards(): lax.all_gather(restored[0], 'range', axis=2, tiled=True)  32.5 us
    all_to_all x1, blocking collectives, shards(): lax.all_to_all(formed, 'chan', split_axis=1, concat_axis=2, tiled=True)  27.7 us
    all_gather x1, waiting for transfers between devices, shards(): shard_piece = lax.all_gather(beam_data, 'range', axis=3, tiled=True)  20.2 us
    all_to_all x1, blocking collectives, shards(): lax.all_to_all(compressed, 'pulse', split_axis=3, concat_axis=2, tiled=True)  17.2 us
    all_to_all x1, blocking collectives, shards(): lax.all_to_all(mixed_real * mixed_real + mixed_imag * mixed_imag, 'pulse'...  16.9 us
  transfers between devices with their start and end apart: 6, of which 6 were waited for; matrix products, arithmetic and copies ran while one was open for 3% of the time, Pallas kernels for 0%

commit v1 on v0

v1 whole, which is shorter than its diff:
```python
import functools
import math

import jax
import jax.numpy as jnp
import numpy as np
from jax import lax
from jax.experimental import pallas as pl
from jax.experimental.pallas import tpu as pltpu
from jax.sharding import PartitionSpec as P

GUARD = 4
TRAIN = 16
NOISE_FLOOR = 0.25
LANES = 128
ROWS = 8
BF = jnp.bfloat16
F32 = jnp.float32
VM = 60 * 1024 * 1024


def dot(a, b):
    return jnp.dot(a, b, preferred_element_type=F32)


def doppler_table(count):
    ids = np.arange(count)
    angle = (np.outer(ids, ids) % count) * (2.0 * np.pi / count)
    scale = 1.0 / math.sqrt(count)
    return jnp.asarray(np.cos(angle) * scale, BF), jnp.asarray(-np.sin(angle) * scale, BF)


def expand(left_ids, left_tag, table, right_ids, right_tag):
    n, m = table.shape
    left = (jnp.asarray(left_ids, jnp.int32)[:, None] == jnp.arange(n)[None, :]).astype(BF)
    right = (jnp.arange(m)[:, None] == jnp.asarray(right_ids, jnp.int32)[None, :]).astype(BF)
    wide = dot(dot(left, table).astype(BF), right)
    same = jnp.asarray(left_tag, jnp.int32)[:, None] == jnp.asarray(right_tag, jnp.int32)[None, :]
    return jnp.where(same, wide, 0.0).astype(BF)


def grid_ids(*sizes):
    return [g.reshape(-1) for g in np.meshgrid(*[np.arange(s) for s in sizes], indexing="ij")]


def call(body, out_shape, name):
    return pl.pallas_call(
        body,
        out_shape=out_shape,
        compiler_params=pltpu.CompilerParams(vmem_limit_bytes=VM),
        name=name,
    )


def form_kernel(w_ref, x_ref, o_ref):
    o_ref[...] = dot(w_ref[...], x_ref[...]).astype(BF)


def range_kernel(blocks, x_ref, f_ref, fi_ref, t_ref, l_ref, li_ref, h_ref, o_ref):
    sources, rows, width = x_ref.shape
    per = width // LANES
    groups = rows // 16
    m_count = sources * per
    tile = []
    for g in range(groups):
        parts = [
            x_ref[s, 16 * g : 16 * g + 16, LANES * j : LANES * j + LANES]
            for s in range(sources)
            for j in range(per)
        ]
        tile.append(jnp.concatenate(parts, axis=0))
    outer = dot(f_ref[...], jnp.concatenate(tile, axis=1))
    tr, ti = t_ref[0], t_ref[1]
    hr, hi = h_ref[0], h_ref[1]
    back = []
    for g in range(groups):
        a = outer[:, LANES * g : LANES * g + LANES].reshape(m_count, 2, ROWS, LANES)
        ar, ai = a[:, 0], a[:, 1]
        b = jnp.concatenate([ar * tr - ai * ti, ar * ti + ai * tr], axis=-1)
        c = dot(b.reshape(m_count * ROWS, 2 * LANES).astype(BF), l_ref[...])
        c = c.reshape(m_count, ROWS, 2 * LANES)
        cr, ci = c[..., :LANES], c[..., LANES:]
        d = jnp.concatenate([cr * hr - ci * hi, cr * hi + ci * hr], axis=-1)
        e = dot(d.reshape(m_count * ROWS, 2 * LANES).astype(BF), li_ref[...])
        e = e.reshape(m_count, ROWS, 2 * LANES)
        er, ei = e[..., :LANES], e[..., LANES:]
        f = jnp.stack([er * tr + ei * ti, ei * tr - er * ti], axis=1)
        back.append(f.reshape(m_count * 16, LANES).astype(BF))
    y = dot(fi_ref[...], jnp.concatenate(back, axis=1)).astype(BF)
    span = m_count // blocks
    for d in range(blocks):
        for j in range(-1, span + 1):
            m = d * span + j
            for g in range(groups):
                if 0 <= m < m_count:
                    v = y[16 * m : 16 * m + 16, LANES * g : LANES * g + LANES]
                else:
                    v = jnp.zeros((16, LANES), BF)
                o_ref[d, 16 * g : 16 * g + 16, LANES * (j + 1) : LANES * (j + 2)] = v


def cfar_kernel(d_ref, x_ref, n_ref, o_ref):
    half = o_ref.shape[0]
    mix = dot(d_ref[...], x_ref[...])
    re, im = mix[:half], mix[half:]
    power = re * re + im * im
    narrow = power.astype(BF)
    for j in range(o_ref.shape[1] // LANES):
        noise = dot(narrow[:, LANES * j : LANES * (j + 3)], n_ref[...])
        own = power[:, LANES * (j + 1) : LANES * (j + 2)]
        o_ref[:, LANES * j : LANES * j + LANES] = (own / (noise + NOISE_FLOOR)).astype(BF)


def cfar_only_kernel(p_ref, n_ref, o_ref):
    narrow = p_ref[...].astype(BF)
    for j in range(o_ref.shape[1] // LANES):
        noise = dot(narrow[:, LANES * j : LANES * (j + 3)], n_ref[...])
        own = p_ref[:, LANES * (j + 1) : LANES * (j + 2)]
        o_ref[:, LANES * j : LANES * j + LANES] = (own / (noise + NOISE_FLOOR)).astype(BF)


def place_kernel(x_ref, o_ref):
    count, _, width = x_ref.shape
    for s in range(count):
        o_ref[:, width * s : width * s + width] = x_ref[s].astype(F32)


def complex_rows(re, im):
    top = np.stack([re, -im], -1)
    low = np.stack([im, re], -1)
    return np.stack([top, low], 1).reshape(2 * re.shape[0], 2 * re.shape[1])


def shards(signal, steering, spectrum):
    beams, chans = steering.shape[1], steering.shape[2]
    _, chan_own, pulse_own, gates = signal.shape
    zs, xs, ys = (lax.axis_size(a) for a in ("chan", "pulse", "range"))
    beam_own = beams // zs
    part = pulse_own // ys
    full = gates * ys
    block = gates // zs
    m_count = full // LANES
    groups = beam_own * part // ROWS
    pulses = pulse_own * xs

    w_real, w_imag = steering[0], steering[1]
    weights = jnp.concatenate(
        [jnp.concatenate([w_real, -w_imag], 1), jnp.concatenate([w_imag, w_real], 1)], 0
    )
    dy, dz, gr, cp, it = grid_ids(ys, zs, groups, 2, ROWS)
    bp = gr * ROWS + it
    left = cp * beams + dz * beam_own + bp // part
    left_pulse = dy * part + bp % part
    sz, ci, ch, pi = grid_ids(zs, 2, chan_own, pulse_own)
    right = ci * chans + sz * chan_own + ch
    form = expand(left, left_pulse, weights, right, pi)

    ms = np.arange(m_count)
    angle = 2.0 * np.pi * (np.outer(ms, ms) % m_count) / m_count
    outer_f = jnp.asarray(complex_rows(np.cos(angle), -np.sin(angle)), BF)
    outer_i = jnp.asarray(complex_rows(np.cos(angle), np.sin(angle)), BF)
    mk, mc, mi = grid_ids(m_count, 2, ROWS)
    outer_f = expand(mk * 2 + mc, mi, outer_f, mk * 2 + mc, mi)
    outer_i = expand(mk * 2 + mc, mi, outer_i, mk * 2 + mc, mi)
    ls = np.arange(LANES)
    angle = 2.0 * np.pi * (np.outer(ls, ls) % LANES) / LANES
    co, si = np.cos(angle), np.sin(angle)
    inner_f = jnp.asarray(np.block([[co, -si], [si, co]]), BF)
    inner_i = jnp.asarray(np.block([[co, si], [-si, co]]), BF)
    angle = 2.0 * np.pi * np.outer(ms, ls) / full
    twiddle = jnp.asarray(np.stack([np.cos(angle), -np.sin(angle)]), F32)
    spread = (2, m_count, ROWS, LANES)
    twiddle = jnp.broadcast_to(twiddle[:, :, None, :], spread)
    response = jnp.swapaxes(spectrum.reshape(2, LANES, m_count), 1, 2) * (1.0 / full)
    response = jnp.broadcast_to(response[:, :, None, :], spread)

    samples = lax.all_to_all(signal, "chan", split_axis=3, concat_axis=0, tiled=True)
    samples = samples.reshape(zs * 2 * chan_own * pulse_own, block)
    rows = 2 * beam_own * part
    formed = call(
        form_kernel, jax.ShapeDtypeStruct((ys * zs * rows, block), BF), "form"
    )(form, samples).reshape(ys * zs, rows, block)
    formed = lax.all_to_all(formed, ("range", "chan"), split_axis=0, concat_axis=0, tiled=True)

    blocks = ys * xs
    own = full // blocks
    padded = own + 2 * LANES
    packed = call(
        functools.partial(range_kernel, blocks),
        jax.ShapeDtypeStruct((blocks, rows, padded), BF),
        "compress",
    )(formed, outer_f, outer_i, twiddle, inner_f, inner_i, response)
    columns = lax.all_to_all(packed, ("range", "pulse"), split_axis=0, concat_axis=0, tiled=True)

    src, dst = np.arange(3 * LANES)[:, None] - LANES, np.arange(LANES)[None, :]
    gap = np.abs(src - dst)
    window = jnp.asarray(((gap > GUARD) & (gap <= GUARD + TRAIN)) / (2.0 * TRAIN), BF)

    dr, di = doppler_table(pulses)
    out_shape = jax.ShapeDtypeStruct((pulses * beam_own, own), BF)
    if 2 * pulses * beam_own <= 1024:
        table = jnp.concatenate([jnp.concatenate([dr, -di], 1), jnp.concatenate([di, dr], 1)], 0)
        oc, oq, ob, of = grid_ids(2, xs, beam_own, pulse_own)
        sy, sx, gr, cp, it = grid_ids(ys, xs, groups, 2, ROWS)
        bp = gr * ROWS + it
        pulse = sx * pulse_own + sy * part + bp % part
        mix = expand(oc * pulses + oq * pulse_own + of, ob, table, cp * pulses + pulse, bp // part)
        found = call(cfar_kernel, out_shape, "cfar")(
            mix, columns.reshape(blocks * rows, padded), window
        )
    else:
        v = columns.reshape(ys, xs, groups, 2, ROWS // part, part, padded)
        v = jnp.transpose(v, (3, 2, 4, 1, 0, 5, 6)).reshape(2, beam_own, pulses, padded)

        def product(t, x):
            return jnp.einsum("fp,bpr->fbr", t, x, preferred_element_type=F32)

        re = product(dr, v[0]) - product(di, v[1])
        im = product(dr, v[1]) + product(di, v[0])
        power = (re * re + im * im).reshape(xs, pulse_own, beam_own, padded)
        power = jnp.swapaxes(power, 1, 2).reshape(pulses * beam_own, padded)
        found = call(cfar_only_kernel, out_shape, "cfar")(power, window)
    found = found.reshape(xs, beam_own * pulse_own, own)
    found = lax.all_to_all(found, "pulse", split_axis=0, concat_axis=0, tiled=True)
    out = call(
        place_kernel, jax.ShapeDtypeStruct((beam_own * pulse_own, gates), F32), "place"
    )(found)
    return out.reshape(beam_own, pulse_own, gates)


def solution(mesh):
    in_specs = (P(None, "chan", "pulse", "range"), P(), P())
    out_specs = P("chan", "pulse", "range")
    return jax.shard_map(shards, mesh=mesh, in_specs=in_specs, out_specs=out_specs, check_vma=False)
```

time: 395 us -> 209 us (0.53); the launches traced: 388 us -> 207 us
  waiting for transfers between devices: 141 us -> 84 us
  blocking collectives: 61.8 us -> 13 us
  local copies, waits for them, and re-layouts: 112 us -> 71.4 us
  other arithmetic: 24.3 us -> 0.04 us
  matrix products: 24.9 us -> 7.78 us
  Pallas kernels: 0 us -> 16.7 us
  between operations: 13.9 us -> 0.2 us
    all_gather x3 -> x0, waiting for transfers between devices: 87.4 us -> none  [the longest x1 34.7 us: shards(): lax.all_gather(restored[1], 'range', axis=2, tiled=True)]
    all_to_all x3 -> x1, blocking collectives: 61.8 us -> 13 us  [shards(): lax.all_to_all(found, 'pulse', split_axis=0, concat_axis=0, tiled=True)]
    all_to_all x1 -> x3, waiting for transfers between devices: 48.2 us -> 84 us  [the longest x1 46.6 us: shards(): lax.all_to_all(signal, 'chan', split_axis=3, concat_axis=0, tiled=True)]
    dot_general x21 -> x4, matrix products: 24.9 us -> 7.78 us  [dot(): return jnp.dot(a, b, preferred_element_type=F32)]
    pallas_call x0 -> x4, Pallas kernels: none -> 16.7 us  [the longest x1 6.94 us: shards(): call(functools.partial(range_kernel, blocks), jax.ShapeDtypeStruct((block...]
    another operation x1 -> x0, local copies, waits for them, and re-layouts: 14 us -> none  [shards(): jnp.stack([sum_real * inverse_scale, sum_imag * inverse_scale])]
    reshape x6 -> x0, local copies, waits for them, and re-layouts: 12.1 us -> none  [the longest x1 6.38 us: shards(): response = spectrum.reshape(2, gate_count, range_count)]
    div x1 -> x0, other arithmetic: 12 us -> none  [shards(): return power_part / (noise_level + NOISE_FLOOR)]
  transfers between devices with their start and end apart: 6 -> 3, of which waited for: 6 -> 3; matrix products, arithmetic and copies ran while one was open for 3% -> 4% of each run, Pallas kernels for 0% -> 0%
where the time goes in v1:
time: 209 us; the launch traced here: 207 us
  waiting for transfers between devices  84 us (40%)
  local copies, waits for them, and re-layouts  71.4 us (34%)
  Pallas kernels  16.7 us (8%)
  starting transfers between devices  14.1 us (7%)
  blocking collectives  13 us (6%)
  matrix products  7.78 us (4%)
    unnamed x37, local copies, waits for them, and re-layouts  50.9 us
    all_to_all x1, waiting for transfers between devices, shards(): lax.all_to_all(signal, 'chan', split_axis=3, concat_axis=0, tiled=True)  46.6 us
    all_to_all x1, waiting for transfers between devices, shards(): lax.all_to_all(formed, ('range', 'chan'), split_axis=0, concat_axis=0, ti...  20.8 us
    all_to_all x1, local copies, waits for them, and re-layouts, shards(): lax.all_to_all(signal, 'chan', split_axis=3, concat_axis=0, tiled=True)  18.5 us
    all_to_all x1, waiting for transfers between devices, shards(): lax.all_to_all(packed, ('range', 'pulse'), split_axis=0, concat_axis=0, t...  16.7 us
    all_to_all x1, blocking collectives, shards(): lax.all_to_all(found, 'pulse', split_axis=0, concat_axis=0, tiled=True)  13 us
    dot_general x4, matrix products, dot(): return jnp.dot(a, b, preferred_element_type=F32)  7.78 us
    pallas_call x1, Pallas kernels, shards(): call(functools.partial(range_kernel, blocks), jax.ShapeDtypeStruct((block...  6.94 us
  transfers between devices with their start and end apart: 3, of which 3 were waited for; matrix products, arithmetic and copies ran while one was open for 4% of the time, Pallas kernels for 0%

profile of v1, /device:TPU:0, one launch (start us, length us, event | category | flops | bytes accessed | tf_op | source)
XLA Modules:
  0.0 207.3 jit_solution(8952435666725432215)
XLA Ops:
  0.0 16.0 %copy.35 = bf16[2,16,8,4096]{1,2,0,3:T(8,128)(2,1)} copy(bf16[2,16,8,4096]{3,2,1,0:T(8,128)(2,1)} %param.27) | data formatting | bytes 4194304 | tf_op args[0]
  16.0 20.3 %reshape.42 = bf16[4,2,131072]{2,1,0:T(2,128)(2,1)} reshape(bf16[4096,2,8,16]{3,2,1,0:T(8,128)(2,1)} %bitcast.21) | data formatting | bytes 4194304
  36.3 0.0 copy-start.16
  36.3 6.5 %all-to-all-start = ((bf16[4,2,131072]{2,1,0:T(2,128)(2,1)}), bf16[4,2,131072]{2,1,0:T(2,128)(2,1)S(1)}, u32[]{:S(2)}, u32[]{:S(2)}) async-start(bf16[4,2,131072]{2,1,0:T(2,128)(2,1)} %reshape.42), calls=%async_computation | async-start | bytes 4194304 | tf_op jit(solution)/shard_map/all_to_all | solution.py:177
  42.8 0.0 copy-done.4
  42.9 0.0 copy-done.8
  42.9 1.6 select_convert_fusion.w_ref
  44.5 46.6 %all-to-all-done = bf16[4,2,131072]{2,1,0:T(2,128)(2,1)S(1)} async-done(((bf16[4,2,131072]{2,1,0:T(2,128)(2,1)}), bf16[4,2,131072]{2,1,0:T(2,128)(2,1)S(1)}, u32[]{:S(2)}, u32[]{:S(2)}) %all-to-all-start) | async-done | bytes 2097184 | tf_op jit(solution)/shard_map/all_to_all | solution.py:177
  91.0 13.5 %reshape.43 = bf16[4096,2,8,16]{3,2,1,0:T(8,128)(2,1)} reshape(bf16[4,2,131072]{2,1,0:T(2,128)(2,1)S(1)} %all-to-all-done) | data formatting | bytes 4194304
  104.5 18.5 %copy.36 = bf16[2,16,8,4,1024]{4,2,1,0,3:T(8,128)(2,1)} copy(bf16[2,16,8,4,1024]{1,2,0,4,3:T(8,128)(2,1)} %bitcast.20) | data formatting | bytes 4194304 | tf_op jit(solution)/shard_map/all_to_all | solution.py:177
  123.0 4.2 %form.1 = bf16[512,1024]{1,0:T(8,128)(2,1)} custom-call(bf16[512,1024]{1,0:T(8,128)(2,1)} %select_convert_fusion.w_ref, bf16[1024,1024]{1,0:T(8,128)(2,1)} %bitcast.22), custom_call_target="tpu_custom_call" | custom-call | tf_op jit(solution)/shard_map/form/pallas_call | solution.py:180
  127.2 3.9 %all-to-all-start.1 = ((bf16[8,64,1024]{2,1,0:T(8,128)(2,1)}), bf16[8,64,1024]{2,1,0:T(8,128)(2,1)S(1)}, u32[]{:S(2)}, u32[]{:S(2)}) async-start(bf16[8,64,1024]{2,1,0:T(8,128)(2,1)} %bitcast.24), calls=%async_computation.1 | async-start | bytes 2097152 | tf_op jit(solution)/shard_map/all_to_all | solution.py:183
  131.1 0.0 copy-done.3
  131.1 0.0 copy-start.5
  131.1 0.1 mul.14
  131.3 0.1 copy.37
  131.4 2.4 %fusion.f_ref = bf16[1024,1024]{1,0:T(8,128)(2,1)} fusion(s32[1024]{0:T(1024)S(1)} %copy-done.8, bf16[128,128]{1,0:T(8,128)(2,1)S(1)} %copy-done.6, s32[1024]{0:T(1024)S(1)} %copy-done.9), kind=kOutput, calls=%fused_computation.2 | convolution fusion | flops 305528832 | bytes 2138112 | tf_op jit(solution)/shard_map/dot_general | solution.py:23
  133.8 2.4 %fusion.1.fi_ref = bf16[1024,1024]{1,0:T(8,128)(2,1)} fusion(s32[1024]{0:T(1024)S(1)} %copy-done.8, bf16[128,128]{1,0:T(8,128)(2,1)S(1)} %copy-done.5, s32[1024]{0:T(1024)S(1)} %copy-done.9), kind=kOutput, calls=%fused_computation.3 | convolution fusion | flops 305528832 | bytes 2138112 | tf_op jit(solution)/shard_map/dot_general | solution.py:23
  136.2 20.8 %all-to-all-done.1.x_ref = bf16[8,64,1024]{2,1,0:T(8,128)(2,1)S(1)} async-done(((bf16[8,64,1024]{2,1,0:T(8,128)(2,1)}), bf16[8,64,1024]{2,1,0:T(8,128)(2,1)S(1)}, u32[]{:S(2)}, u32[]{:S(2)}) %all-to-all-start.1) | async-done | bytes 1048608 | tf_op jit(solution)/shard_map/all_to_all | solution.py:183
  157.0 0.9 broadcast_in_dim.20.h_ref
  158.0 0.8 broadcast_in_dim.19.t_ref
  158.8 0.0 copy-done.1
  158.8 6.9 %compress.1 = bf16[8,64,1280]{2,1,0:T(8,128)(2,1)} custom-call(bf16[8,64,1024]{2,1,0:T(8,128)(2,1)} %copy-done.1, bf16[1024,1024]{1,0:T(8,128)(2,1)} %fusion.f_ref, bf16[1024,1024]{1,0:T(8,128)(2,1)} %fusion.1.fi_ref, f32[2,64,8,128]{3,2,1,0:T(8,128)} %broadcast_in_dim.19.t_ref, bf16[256,256]{1,0:T(8,128)(2,1)} %constant.45.clone.l_ref, ...), custom_call_target="tpu_custom_call" | custom-call | tf_op jit(solution)/shard_map/compress/pallas_call | solution.py:188
  165.7 0.0 copy-start.13
  165.7 0.0 copy-start.14
  165.8 3.7 %all-to-all-start.2 = ((bf16[8,64,1280]{2,1,0:T(8,128)(2,1)}), bf16[8,64,1280]{2,1,0:T(8,128)(2,1)S(1)}, u32[]{:S(2)}, u32[]{:S(2)}) async-start(bf16[8,64,1280]{2,1,0:T(8,128)(2,1)} %compress.1), calls=%async_computation.2 | async-start | bytes 2621440 | tf_op jit(solution)/shard_map/all_to_all | solution.py:193
  169.5 1.4 fusion.2.d_ref
  170.9 16.7 %all-to-all-done.2 = bf16[8,64,1280]{2,1,0:T(8,128)(2,1)S(1)} async-done(((bf16[8,64,1280]{2,1,0:T(8,128)(2,1)}), bf16[8,64,1280]{2,1,0:T(8,128)(2,1)S(1)}, u32[]{:S(2)}, u32[]{:S(2)}) %all-to-all-start.2) | async-done | bytes 1310752 | tf_op jit(solution)/shard_map/all_to_all | solution.py:193
  187.6 1.1 copy-done
  188.7 3.5 %cfar.1 = bf16[256,1024]{1,0:T(8,128)(2,1)} custom-call(bf16[512,512]{1,0:T(8,128)(2,1)} %fusion.2.d_ref, bf16[512,1280]{1,0:T(8,128)(2,1)} %bitcast.23, bf16[384,128]{1,0:T(8,128)(2,1)} %constant.48.clone.n_ref), custom_call_target="tpu_custom_call" | custom-call | tf_op jit(solution)/shard_map/cfar/pallas_call | solution.py:208
  192.2 13.0 %all_to_all.30.x_ref = bf16[4,64,1024]{2,1,0:T(8,128)(2,1)} all-to-all(bf16[4,64,1024]{2,1,0:T(8,128)(2,1)} %bitcast.25), channel_id=1, replica_groups=mesh['chan'=4,'pulse'=4,'range'=2] {'pulse'}, dimensions={0} | all-to-all | bytes 1048576 | tf_op jit(solution)/shard_map/all_to_all | solution.py:224
  205.2 2.1 %place.1 = f32[64,4096]{1,0:T(8,128)} custom-call(bf16[4,64,1024]{2,1,0:T(8,128)(2,1)} %all_to_all.30.x_ref), custom_call_target="tpu_custom_call" | custom-call | tf_op jit(solution)/shard_map/place/pallas_call | solution.py:225
  (28 shorter events, 0.1 us)
Async XLA Ops:
  36.3 6.5 %copy-start.4 = (bf16[2,32,64]{2,1,0:T(8,128)(2,1)S(1)}, bf16[2,32,64]{2,1,0:T(8,128)(2,1)}, u32[]{:S(2)}) copy-start(bf16[2,32,64]{2,1,0:T(8,128)(2,1)} %param.28) | copy-start | bytes 24580
  36.3 6.5 %copy-start.8 = (s32[1024]{0:T(1024)S(1)}, s32[1024]{0:T(1024)}, u32[]{:S(2)}) copy-start(s32[1024]{0:T(1024)} %constant.41.clone) | copy-start | bytes 12292
  36.3 6.5 %copy-start.10 = (s32[1024]{0:T(1024)S(1)}, s32[1024]{0:T(1024)}, u32[]{:S(2)}) copy-start(s32[1024]{0:T(1024)} %constant.39.clone) | copy-start | bytes 12292
  36.3 6.6 %copy-start.15 = (s32[512]{0:T(512)S(1)}, s32[512]{0:T(512)}, u32[]{:S(2)}) copy-start(s32[512]{0:T(512)} %constant.38.clone) | copy-start | bytes 6148
  36.3 6.6 %copy-start.16 = (s32[512]{0:T(512)S(1)}, s32[512]{0:T(512)}, u32[]{:S(2)}) copy-start(s32[512]{0:T(512)} %constant.40.clone) | copy-start | bytes 6148
  36.3 54.7 %all-to-all-start = ((bf16[4,2,131072]{2,1,0:T(2,128)(2,1)}), bf16[4,2,131072]{2,1,0:T(2,128)(2,1)S(1)}, u32[]{:S(2)}, u32[]{:S(2)}) async-start(bf16[4,2,131072]{2,1,0:T(2,128)(2,1)} %reshape.42), calls=%async_computation | async-start | bytes 4194304 | tf_op jit(solution)/shard_map/all_to_all | solution.py:177
  127.2 3.9 %copy-start.3 = (f32[2,8192]{1,0:T(2,128)S(1)}, f32[2,8192]{1,0:T(2,128)}, u32[]{:S(2)}) copy-start(f32[2,8192]{1,0:T(2,128)} %param.29) | copy-start | bytes 196612
  127.2 4.2 %copy-start.6 = (bf16[128,128]{1,0:T(8,128)(2,1)S(1)}, bf16[128,128]{1,0:T(8,128)(2,1)}, u32[]{:S(2)}) copy-start(bf16[128,128]{1,0:T(8,128)(2,1)} %constant.42.clone) | copy-start | bytes 98308
  127.2 4.2 %copy-start.9 = (s32[1024]{0:T(1024)S(1)}, s32[1024]{0:T(1024)}, u32[]{:S(2)}) copy-start(s32[1024]{0:T(1024)} %constant.44.clone) | copy-start | bytes 12292
  127.2 29.8 %all-to-all-start.1 = ((bf16[8,64,1024]{2,1,0:T(8,128)(2,1)}), bf16[8,64,1024]{2,1,0:T(8,128)(2,1)S(1)}, u32[]{:S(2)}, u32[]{:S(2)}) async-start(bf16[8,64,1024]{2,1,0:T(8,128)(2,1)} %bitcast.24), calls=%async_computation.1 | async-start | bytes 2097152 | tf_op jit(solution)/shard_map/all_to_all | solution.py:183
  131.1 2.7 %copy-start.5 = (bf16[128,128]{1,0:T(8,128)(2,1)S(1)}, bf16[128,128]{1,0:T(8,128)(2,1)}, u32[]{:S(2)}) copy-start(bf16[128,128]{1,0:T(8,128)(2,1)} %constant.43.clone) | copy-start | bytes 98308
  133.8 24.1 %copy-start.2 = (f32[2,64,128]{2,1,0:T(8,128)S(1)}, f32[2,64,128]{2,1,0:T(8,128)}, u32[]{:S(2)}) copy-start(f32[2,64,128]{2,1,0:T(8,128)} %constant.47.clone) | copy-start | bytes 196612
  157.0 1.8 copy-start.1
  165.7 3.8 %copy-start.7 = (bf16[64,64]{1,0:T(8,128)(2,1)S(1)}, bf16[64,64]{1,0:T(8,128)(2,1)}, u32[]{:S(2)}) copy-start(bf16[64,64]{1,0:T(8,128)(2,1)} %constant.58) | copy-start | bytes 24580
  165.7 3.8 %copy-start.11 = (s32[512]{0:T(512)S(1)}, s32[512]{0:T(512)}, u32[]{:S(2)}) copy-start(s32[512]{0:T(512)} %constant.51.clone) | copy-start | bytes 6148
  165.7 3.8 %copy-start.12 = (s32[512]{0:T(512)S(1)}, s32[512]{0:T(512)}, u32[]{:S(2)}) copy-start(s32[512]{0:T(512)} %constant.52.clone) | copy-start | bytes 6148
  165.7 3.8 %copy-start.13 = (s32[512]{0:T(512)S(1)}, s32[512]{0:T(512)}, u32[]{:S(2)}) copy-start(s32[512]{0:T(512)} %constant.53.clone) | copy-start | bytes 6148
  165.7 3.8 %copy-start.14 = (s32[512]{0:T(512)S(1)}, s32[512]{0:T(512)}, u32[]{:S(2)}) copy-start(s32[512]{0:T(512)} %constant.54.clone) | copy-start | bytes 6148
  165.8 21.8 %all-to-all-start.2 = ((bf16[8,64,1280]{2,1,0:T(8,128)(2,1)}), bf16[8,64,1280]{2,1,0:T(8,128)(2,1)S(1)}, u32[]{:S(2)}, u32[]{:S(2)}) async-start(bf16[8,64,1280]{2,1,0:T(8,128)(2,1)} %compress.1), calls=%async_computation.2 | async-start | bytes 2621440 | tf_op jit(solution)/shard_map/all_to_all | solution.py:193
  187.6 1.1 copy-start

commit v2 on v1

--- a/solution.py
+++ b/solution.py
@@ -100,15 +100,17 @@
 
 
 def cfar_kernel(d_ref, x_ref, n_ref, o_ref):
-    half = o_ref.shape[0]
-    mix = dot(d_ref[...], x_ref[...])
+    half = d_ref.shape[0] // 2
+    mix = dot(d_ref[...], x_ref[...].reshape(d_ref.shape[1], x_ref.shape[-1]))
     re, im = mix[:half], mix[half:]
     power = re * re + im * im
     narrow = power.astype(BF)
-    for j in range(o_ref.shape[1] // LANES):
+    shape = o_ref.shape[:-1] + (LANES,)
+    for j in range(o_ref.shape[-1] // LANES):
         noise = dot(narrow[:, LANES * j : LANES * (j + 3)], n_ref[...])
         own = power[:, LANES * (j + 1) : LANES * (j + 2)]
-        o_ref[:, LANES * j : LANES * j + LANES] = (own / (noise + NOISE_FLOOR)).astype(BF)
+        found = (own / (noise + NOISE_FLOOR)).astype(BF)
+        o_ref[..., LANES * j : LANES * j + LANES] = found.reshape(shape)
 
 
 def cfar_only_kernel(p_ref, n_ref, o_ref):
@@ -131,7 +133,7 @@
     return np.stack([top, low], 1).reshape(2 * re.shape[0], 2 * re.shape[1])
 
 
-def shards(signal, steering, spectrum):
+def shards_split(signal, steering, spectrum):
     beams, chans = steering.shape[1], steering.shape[2]
     _, chan_own, pulse_own, gates = signal.shape
     zs, xs, ys = (lax.axis_size(a) for a in ("chan", "pulse", "range"))
@@ -228,6 +230,225 @@
     return out.reshape(beam_own, pulse_own, gates)
 
 
+MESH = pl.DeviceIdType.MESH
+
+
+def widen(left, right, table):
+    n, m = table.shape
+    r, c = left.shape[1], right.shape[1]
+    pick_l = (left[0] == lax.broadcasted_iota(jnp.int32, (r, n), 1)).astype(F32).astype(BF)
+    pick_r = (right[0] == lax.broadcasted_iota(jnp.int32, (m, c), 0)).astype(F32).astype(BF)
+    wide = dot(dot(pick_l, table[...]).astype(BF), pick_r)
+    return jnp.where(left[1] == right[1], wide, 0.0).astype(BF)
+
+
+def chain_kernel(
+    sizes, sig, w_l, w_r, w_t, f_l, f_r, f_t, fi_t, tw, inf, ini, resp, d_l, d_r, d_t, win, out,
+    recv1, send2, recv2, send3, recv3, send4, recv4, wide_w, wide_f, wide_i, wide_d, spread,
+    acc, own_sem, s1, r1, s2, r2, s3, r3, s4, r4,
+):
+    zs, ys, xs = sizes
+    block = recv1.shape[2]
+    z, y, x = (lax.axis_index(a) for a in ("chan", "range", "pulse"))
+
+    def zy(i):
+        return {"range": lax.div(i, zs), "chan": lax.rem(i, zs)}
+
+    def xy(i):
+        return {"range": lax.div(i, xs), "pulse": lax.rem(i, xs)}
+
+    n2, n3 = ys * zs, ys * xs
+    me2, me3 = y * zs + z, y * xs + x
+    barrier = pltpu.get_barrier_semaphore()
+    peers = 0
+    for k in range(1, n2):
+        pl.semaphore_signal(
+            barrier, inc=1, device_id=zy(lax.rem(me2 + k, n2)), device_id_type=MESH
+        )
+        peers += 1
+    for dy in range(ys):
+        for dx in range(1, xs):
+            target = {"range": lax.rem(y + dy, ys), "pulse": lax.rem(x + dx, xs)}
+            pl.semaphore_signal(barrier, inc=1, device_id=target, device_id_type=MESH)
+            peers += 1
+    pl.semaphore_wait(barrier, peers)
+
+    def piece(i):
+        return sig.at[:, pl.ds(pl.multiple_of(i * block, block), block)]
+
+    def push(src, dst, send, recv, k, target):
+        copy = pltpu.make_async_remote_copy(
+            src_ref=src, dst_ref=dst, send_sem=send.at[k], recv_sem=recv.at[k],
+            device_id=target, device_id_type=MESH,
+        )
+        copy.start()
+        return copy
+
+    first = []
+    for k in range(1, zs):
+        to = lax.rem(z + k, zs)
+        first.append(push(piece(to), recv1.at[z], s1, r1, k, {"chan": to}))
+    mine = pltpu.make_async_copy(piece(z), recv1.at[z], own_sem)
+    mine.start()
+
+    for s in range(zs):
+        wide_w[s] = widen(w_l, w_r[s], w_t)
+    wide_f[...] = widen(f_l, f_r, f_t)
+    wide_i[...] = widen(f_l, f_r, fi_t)
+    wide_d[...] = widen(d_l, d_r, d_t)
+    m_count = tw.shape[1]
+    for i in range(2):
+        spread[i] = jnp.broadcast_to(tw[i][:, None, :], (m_count, ROWS, LANES))
+        spread[2 + i] = jnp.broadcast_to(resp[i][:, None, :], (m_count, ROWS, LANES))
+
+    mine.wait()
+    acc[...] = dot(wide_w[z], recv1[z])
+    for k in range(1, zs):
+        src = lax.rem(z + zs - k, zs)
+        first[k - 1].wait_recv()
+        acc[...] += dot(wide_w[src], recv1[src])
+    send2[...] = acc[...].astype(BF).reshape(send2.shape)
+    second = []
+    for k in range(1, n2):
+        to = lax.rem(me2 + k, n2)
+        second.append(push(send2.at[to], recv2.at[me2], s2, r2, k, zy(to)))
+    recv2[me2] = send2[me2]
+    for copy in second:
+        copy.wait_recv()
+
+    range_kernel(
+        n3, recv2, wide_f, wide_i, spread.at[pl.ds(0, 2)], inf, ini, spread.at[pl.ds(2, 2)], send3
+    )
+    third = []
+    for k in range(1, n3):
+        to = lax.rem(me3 + k, n3)
+        third.append(push(send3.at[to], recv3.at[me3], s3, r3, k, xy(to)))
+    recv3[me3] = send3[me3]
+    for copy in third:
+        copy.wait_recv()
+
+    cfar_kernel(wide_d, recv3, win, send4)
+    fourth = []
+    for k in range(1, xs):
+        to = lax.rem(x + k, xs)
+        fourth.append(push(send4.at[to], recv4.at[x], s4, r4, k, {"pulse": to}))
+    recv4[x] = send4[x]
+    for copy in fourth:
+        copy.wait_recv()
+    place_kernel(recv4, out)
+    for copy in first + second + third + fourth:
+        copy.wait_send()
+
+
+def ids_pair(ids, tags):
+    return np.stack([ids, tags]).astype(np.int32)
+
+
+def shards_chain(signal, steering, spectrum):
+    beams, chans = steering.shape[1], steering.shape[2]
+    _, chan_own, pulse_own, gates = signal.shape
+    zs, xs, ys = (lax.axis_size(a) for a in ("chan", "pulse", "range"))
+    beam_own = beams // zs
+    part = pulse_own // ys
+    full = gates * ys
+    block = gates // zs
+    m_count = full // LANES
+    groups = beam_own * part // ROWS
+    pulses = pulse_own * xs
+    rows = 2 * beam_own * part
+    blocks = ys * xs
+    own = full // blocks
+    padded = own + 2 * LANES
+
+    w_real, w_imag = steering[0], steering[1]
+    weights = jnp.concatenate(
+        [jnp.concatenate([w_real, -w_imag], 1), jnp.concatenate([w_imag, w_real], 1)], 0
+    )
+    dy, dz, gr, cp, it = grid_ids(ys, zs, groups, 2, ROWS)
+    bp = gr * ROWS + it
+    w_l = ids_pair(cp * beams + dz * beam_own + bp // part, dy * part + bp % part)[:, :, None]
+    w_r = []
+    for s in range(zs):
+        ci, ch, pi = grid_ids(2, chan_own, pulse_own)
+        w_r.append(ids_pair(ci * chans + s * chan_own + ch, pi)[:, None, :])
+    w_r = np.stack(w_r)
+
+    ms = np.arange(m_count)
+    angle = 2.0 * np.pi * (np.outer(ms, ms) % m_count) / m_count
+    outer_f = jnp.asarray(complex_rows(np.cos(angle), -np.sin(angle)), BF)
+    outer_i = jnp.asarray(complex_rows(np.cos(angle), np.sin(angle)), BF)
+    mk, mc, mi = grid_ids(m_count, 2, ROWS)
+    f_ids = ids_pair(mk * 2 + mc, mi)
+    ls = np.arange(LANES)
+    angle = 2.0 * np.pi * (np.outer(ls, ls) % LANES) / LANES
+    co, si = np.cos(angle), np.sin(angle)
+    inner_f = jnp.asarray(np.block([[co, -si], [si, co]]), BF)
+    inner_i = jnp.asarray(np.block([[co, si], [-si, co]]), BF)
+    angle = 2.0 * np.pi * np.outer(ms, ls) / full
+    twiddle = jnp.asarray(np.stack([np.cos(angle), -np.sin(angle)]), F32)
+    response = jnp.swapaxes(spectrum.reshape(2, LANES, m_count), 1, 2) * (1.0 / full)
+
+    src, dst = np.arange(3 * LANES)[:, None] - LANES, np.arange(LANES)[None, :]
+    gap = np.abs(src - dst)
+    window = jnp.asarray(((gap > GUARD) & (gap <= GUARD + TRAIN)) / (2.0 * TRAIN), BF)
+    dr, di = doppler_table(pulses)
+    table = jnp.concatenate([jnp.concatenate([dr, -di], 1), jnp.concatenate([di, dr], 1)], 0)
+    oc, oq, ob, of = grid_ids(2, xs, beam_own, pulse_own)
+    sy, sx, gr, cp, it = grid_ids(ys, xs, groups, 2, ROWS)
+    bp = gr * ROWS + it
+    pulse = sx * pulse_own + sy * part + bp % part
+    d_l = ids_pair(oc * pulses + oq * pulse_own + of, ob)[:, :, None]
+    d_r = ids_pair(cp * pulses + pulse, bp // part)[:, None, :]
+
+    depth = 2 * chan_own * pulse_own
+    kernel_rows = 2 * beams * pulse_own
+    cells = beam_own * pulse_own
+    vmem = pl.BlockSpec(memory_space=pltpu.VMEM)
+    dma = pltpu.SemaphoreType.DMA
+    out = pl.pallas_call(
+        functools.partial(chain_kernel, (zs, ys, xs)),
+        out_shape=jax.ShapeDtypeStruct((cells, gates), F32),
+        in_specs=[pl.BlockSpec(memory_space=pl.ANY)] + [vmem] * 15,
+        out_specs=vmem,
+        scratch_shapes=[
+            pltpu.VMEM((zs, depth, block), BF),
+            pltpu.VMEM((ys * zs, rows, block), BF),
+            pltpu.VMEM((ys * zs, rows, block), BF),
+            pltpu.VMEM((blocks, rows, padded), BF),
+            pltpu.VMEM((blocks, rows, padded), BF),
+            pltpu.VMEM((xs, cells, own), BF),
+            pltpu.VMEM((xs, cells, own), BF),
+            pltpu.VMEM((zs, kernel_rows, depth), BF),
+            pltpu.VMEM((m_count * 16, m_count * 16), BF),
+            pltpu.VMEM((m_count * 16, m_count * 16), BF),
+            pltpu.VMEM((2 * pulses * beam_own, blocks * rows), BF),
+            pltpu.VMEM((4, m_count, ROWS, LANES), F32),
+            pltpu.VMEM((kernel_rows, block), F32),
+            dma,
+            dma((zs,)), dma((zs,)),
+            dma((ys * zs,)), dma((ys * zs,)),
+            dma((blocks,)), dma((blocks,)),
+            dma((xs,)), dma((xs,)),
+        ],
+        compiler_params=pltpu.CompilerParams(
+            collective_id=0, has_side_effects=True, vmem_limit_bytes=VM
+        ),
+        name="chain",
+    )(
+        signal.reshape(depth, gates), w_l, w_r, weights,
+        f_ids[:, :, None], f_ids[:, None, :], outer_f, outer_i,
+        twiddle, inner_f, inner_i, response, d_l, d_r, table, window,
+    )
+    return out.reshape(beam_own, pulse_own, gates)
+
+
+def shards(signal, steering, spectrum):
+    pulses = signal.shape[2] * lax.axis_size("pulse")
+    beam_own = steering.shape[1] // lax.axis_size("chan")
+    small = 2 * pulses * beam_own <= 1024
+    return (shards_chain if small else shards_split)(signal, steering, spectrum)
+
+
 def solution(mesh):
     in_specs = (P(None, "chan", "pulse", "range"), P(), P())
     out_specs = P("chan", "pulse", "range")

time: 209 us -> 113 us (0.54)
  the two profiles are of different devices: /device:TPU:0 before, /device:TPU:19 now
where the time goes in v2:
time: 113 us
  Pallas kernels  107 us (95%)
  local copies, waits for them, and re-layouts  3.84 us (3%)
  other arithmetic  2.25 us (2%)
    pallas_call x1, Pallas kernels, shards_chain(): pl.pallas_call(functools.partial(chain_kernel, (zs, ys, xs)), out_shape=j...  107 us
    unnamed x1, local copies, waits for them, and re-layouts  2.27 us

profile of v2, /device:TPU:19, one launch (start us, length us, event | category | flops | bytes accessed | tf_op | source)
XLA Modules:
  0.0 112.8 jit_solution(8373749941418156525)
XLA Ops:
  0.0 0.7 fusion
  0.7 0.7 slice_bitcast_fusion
  1.4 0.7 maximum_maximum_fusion.w_t
  2.1 0.9 broadcast_multiply_fusion
  3.0 0.1 mul.12
  3.1 0.7 copy.18
  3.8 106.7 %chain.1 = f32[64,4096]{1,0:T(8,128)} custom-call(bf16[256,4096]{1,0:T(8,128)(2,1)} %bitcast.10, s32[2,512,1]{2,1,0:T(8,128)} %constant.38.clone.w_l, s32[4,2,1,256]{3,2,1,0:T(1,128)} %constant.39.clone.w_r, bf16[64,128]{1,0:T(8,128)(2,1)} %maximum_maximum_fusion.w_t, s32[2,1024,1]{2,1,0:T(8,128)} %constant.40.clone.f_l, s32[2,1,1024]{2,1,0:T(1,128)} %constant.41.clone.f_r, ...), custom_call_target="tpu_custom_call" | custom-call | tf_op jit(solution)/shard_map/chain/pallas_call | solution.py:408
  110.5 2.3 %copy.20 = f32[8,8,4096]{2,1,0:T(8,128)} copy(f32[8,8,4096]{2,1,0:T(8,128)} %bitcast.9) | data formatting | bytes 2097152

commit v3 on v2

--- a/solution.py
+++ b/solution.py
@@ -14,6 +14,7 @@
 NOISE_FLOOR = 0.25
 LANES = 128
 ROWS = 8
+CHUNKS = 8
 BF = jnp.bfloat16
 F32 = jnp.float32
 VM = 60 * 1024 * 1024
@@ -244,11 +245,11 @@
 
 def chain_kernel(
     sizes, sig, w_l, w_r, w_t, f_l, f_r, f_t, fi_t, tw, inf, ini, resp, d_l, d_r, d_t, win, out,
-    recv1, send2, recv2, send3, recv3, send4, recv4, wide_w, wide_f, wide_i, wide_d, spread,
-    acc, own_sem, s1, r1, s2, r2, s3, r3, s4, r4,
+    recv1, own1, sendp, recvp, send2, recv2, send3, recv3, send4, recv4, wide_w, wide_f, wide_i,
+    wide_d, spread, acc, own_sem, s1, r1, sp, rp, s2, r2, s3, r3, s4, r4,
 ):
     zs, ys, xs = sizes
-    block = recv1.shape[2]
+    chunks, _, block = recv1.shape
     z, y, x = (lax.axis_index(a) for a in ("chan", "range", "pulse"))
 
     def zy(i):
@@ -276,23 +277,36 @@
     def piece(i):
         return sig.at[:, pl.ds(pl.multiple_of(i * block, block), block)]
 
-    def push(src, dst, send, recv, k, target):
-        copy = pltpu.make_async_remote_copy(
-            src_ref=src, dst_ref=dst, send_sem=send.at[k], recv_sem=recv.at[k],
+    def plan(src, dst, send, recv, target):
+        return pltpu.make_async_remote_copy(
+            src_ref=src, dst_ref=dst, send_sem=send, recv_sem=recv,
             device_id=target, device_id_type=MESH,
         )
+
+    def push(src, dst, send, recv, k, target):
+        copy = plan(src, dst, send.at[k], recv.at[k], target)
         copy.start()
         return copy
 
-    first = []
-    for k in range(1, zs):
-        to = lax.rem(z + k, zs)
-        first.append(push(piece(to), recv1.at[z], s1, r1, k, {"chan": to}))
-    mine = pltpu.make_async_copy(piece(z), recv1.at[z], own_sem)
-    mine.start()
-
-    for s in range(zs):
-        wide_w[s] = widen(w_l, w_r[s], w_t)
+    half = lax.div(z, 2)
+    hub, edge = 1 + half, 3 * half
+    is_hub = z == hub
+    is_edge = z == edge
+    raw = [plan(piece(c), recv1.at[c], s1.at[c], r1.at[c], {"chan": hub}) for c in range(chunks)]
+    mine = [pltpu.make_async_copy(piece(c), own1.at[c], own_sem.at[c]) for c in range(chunks)]
+
+    @pl.when(is_edge)
+    def _():
+        for c in range(chunks):
+            raw[c].start()
+
+    @pl.when(is_hub)
+    def _():
+        for c in range(chunks):
+            mine[c].start()
+        wide_w[0] = widen(w_l, w_r.at[hub], w_t)
+        wide_w[1] = widen(w_l, w_r.at[edge], w_t)
+
     wide_f[...] = widen(f_l, f_r, f_t)
     wide_i[...] = widen(f_l, f_r, fi_t)
     wide_d[...] = widen(d_l, d_r, d_t)
@@ -301,20 +315,70 @@
         spread[i] = jnp.broadcast_to(tw[i][:, None, :], (m_count, ROWS, LANES))
         spread[2 + i] = jnp.broadcast_to(resp[i][:, None, :], (m_count, ROWS, LANES))
 
-    mine.wait()
-    acc[...] = dot(wide_w[z], recv1[z])
-    for k in range(1, zs):
-        src = lax.rem(z + zs - k, zs)
-        first[k - 1].wait_recv()
-        acc[...] += dot(wide_w[src], recv1[src])
-    send2[...] = acc[...].astype(BF).reshape(send2.shape)
-    second = []
-    for k in range(1, n2):
-        to = lax.rem(me2 + k, n2)
-        second.append(push(send2.at[to], recv2.at[me2], s2, r2, k, zy(to)))
-    recv2[me2] = send2[me2]
-    for copy in second:
-        copy.wait_recv()
+    other_y = [lax.rem(y + k, ys) for k in range(1, ys)]
+    half_rows = sendp.shape[1]
+
+    def swap(c):
+        return plan(sendp.at[c], recvp.at[c], sp.at[c], rp.at[c], {"chan": 3 - hub})
+
+    def hand(c, i, to_y, zz, to_z):
+        k = i * chunks + c
+        slot = y * chunks + c
+        return plan(
+            send2.at[c, to_y, zz], recv2.at[slot], s2.at[k], r2.at[slot],
+            {"range": to_y, "chan": to_z},
+        )
+
+    def hands(c):
+        found = [hand(c, 0, y, half, edge)]
+        for i, to_y in enumerate(other_y):
+            found.append(hand(c, 1 + 2 * i, to_y, half, edge))
+            found.append(hand(c, 2 + 2 * i, to_y, 1 - half, hub))
+        return found
+
+    def arrived(src_y, c):
+        slot = src_y * chunks + c
+        plan(
+            send2.at[c, y, 0], recv2.at[slot], s2.at[0], r2.at[slot],
+            {"range": src_y, "chan": hub},
+        ).wait_recv()
+
+    @pl.when(is_hub)
+    def _():
+        near = pl.ds(pl.multiple_of(half * half_rows, half_rows), half_rows)
+        far = pl.ds(pl.multiple_of((1 - half) * half_rows, half_rows), half_rows)
+
+        def finish(c):
+            swap(c).wait_recv()
+            total = (acc[c] + recvp[c].astype(F32)).astype(BF)
+            send2[c] = total.reshape(send2.shape[1:])
+            for copy in hands(c):
+                copy.start()
+            recv2[y * chunks + c] = send2[c, y, 1 - half]
+
+        for c in range(chunks):
+            mine[c].wait()
+            raw[c].wait_recv()
+            a, b = own1[c], recv1[c]
+            sendp[c] = (dot(wide_w[0, far], a) + dot(wide_w[1, far], b)).astype(BF)
+            swap(c).start()
+            acc[c] = dot(wide_w[0, near], a) + dot(wide_w[1, near], b)
+            if c > 0:
+                finish(c - 1)
+        finish(chunks - 1)
+        for c in range(chunks):
+            for to_y in other_y:
+                arrived(to_y, c)
+            swap(c).wait_send()
+            for copy in hands(c):
+                copy.wait_send()
+
+    @pl.when(is_edge)
+    def _():
+        for c in range(chunks):
+            for src_y in [y] + other_y:
+                arrived(src_y, c)
+            raw[c].wait_send()
 
     range_kernel(
         n3, recv2, wide_f, wide_i, spread.at[pl.ds(0, 2)], inf, ini, spread.at[pl.ds(2, 2)], send3
@@ -336,7 +400,7 @@
     for copy in fourth:
         copy.wait_recv()
     place_kernel(recv4, out)
-    for copy in first + second + third + fourth:
+    for copy in third + fourth:
         copy.wait_send()
 
 
@@ -351,7 +415,8 @@
     beam_own = beams // zs
     part = pulse_own // ys
     full = gates * ys
-    block = gates // zs
+    chunks = CHUNKS
+    block = gates // chunks
     m_count = full // LANES
     groups = beam_own * part // ROWS
     pulses = pulse_own * xs
@@ -364,7 +429,8 @@
     weights = jnp.concatenate(
         [jnp.concatenate([w_real, -w_imag], 1), jnp.concatenate([w_imag, w_real], 1)], 0
     )
-    dy, dz, gr, cp, it = grid_ids(ys, zs, groups, 2, ROWS)
+    dh, dy, dz, gr, cp, it = grid_ids(2, ys, 2, groups, 2, ROWS)
+    dz = dz + 2 * dh
     bp = gr * ROWS + it
     w_l = ids_pair(cp * beams + dz * beam_own + bp // part, dy * part + bp % part)[:, :, None]
     w_r = []
@@ -411,22 +477,26 @@
         in_specs=[pl.BlockSpec(memory_space=pl.ANY)] + [vmem] * 15,
         out_specs=vmem,
         scratch_shapes=[
-            pltpu.VMEM((zs, depth, block), BF),
-            pltpu.VMEM((ys * zs, rows, block), BF),
-            pltpu.VMEM((ys * zs, rows, block), BF),
+            pltpu.VMEM((chunks, depth, block), BF),
+            pltpu.VMEM((chunks, depth, block), BF),
+            pltpu.VMEM((chunks, kernel_rows // 2, block), BF),
+            pltpu.VMEM((chunks, kernel_rows // 2, block), BF),
+            pltpu.VMEM((chunks, ys, 2, rows, block), BF),
+            pltpu.VMEM((ys * chunks, rows, block), BF),
             pltpu.VMEM((blocks, rows, padded), BF),
             pltpu.VMEM((blocks, rows, padded), BF),
             pltpu.VMEM((xs, cells, own), BF),
             pltpu.VMEM((xs, cells, own), BF),
-            pltpu.VMEM((zs, kernel_rows, depth), BF),
+            pltpu.VMEM((2, kernel_rows, depth), BF),
             pltpu.VMEM((m_count * 16, m_count * 16), BF),
             pltpu.VMEM((m_count * 16, m_count * 16), BF),
             pltpu.VMEM((2 * pulses * beam_own, blocks * rows), BF),
             pltpu.VMEM((4, m_count, ROWS, LANES), F32),
-            pltpu.VMEM((kernel_rows, block), F32),
-            dma,
-            dma((zs,)), dma((zs,)),
-            dma((ys * zs,)), dma((ys * zs,)),
+            pltpu.VMEM((chunks, kernel_rows // 2, block), F32),
+            dma((chunks,)),
+            dma((chunks,)), dma((chunks,)),
+            dma((chunks,)), dma((chunks,)),
+            dma(((2 * ys - 1) * chunks,)), dma((ys * chunks,)),
             dma((blocks,)), dma((blocks,)),
             dma((xs,)), dma((xs,)),
         ],
@@ -445,7 +515,7 @@
 def shards(signal, steering, spectrum):
     pulses = signal.shape[2] * lax.axis_size("pulse")
     beam_own = steering.shape[1] // lax.axis_size("chan")
-    small = 2 * pulses * beam_own <= 1024
+    small = 2 * pulses * beam_own <= 1024 and lax.axis_size("chan") == 4
     return (shards_chain if small else shards_split)(signal, steering, spectrum)
 
 

time: 113 us -> 99.1 us (0.88)
  the two profiles are of different devices: /device:TPU:19 before, /device:TPU:0 now
where the time goes in v3:
time: 99.1 us; the launch traced here: 97.6 us
  Pallas kernels  91.5 us (92%)
  local copies, waits for them, and re-layouts  3.84 us (4%)
  other arithmetic  2.25 us (2%)
    pallas_call x1, Pallas kernels, shards_chain(): pl.pallas_call(functools.partial(chain_kernel, (zs, ys, xs)), out_shape=j...  91.5 us
    unnamed x1, local copies, waits for them, and re-layouts  2.27 us

profile of v3, /device:TPU:0, one launch (start us, length us, event | category | flops | bytes accessed | tf_op | source)
XLA Modules:
  0.0 97.6 jit_solution(300538742252242753)
XLA Ops:
  0.0 0.7 fusion
  0.7 0.7 slice_bitcast_fusion
  1.4 0.7 maximum_maximum_fusion.w_t
  2.1 0.9 broadcast_multiply_fusion
  3.0 0.1 mul.12
  3.1 0.7 copy.18
  3.8 91.5 %chain.1 = f32[64,4096]{1,0:T(8,128)} custom-call(bf16[256,4096]{1,0:T(8,128)(2,1)} %bitcast.10, s32[2,512,1]{2,1,0:T(8,128)} %constant.38.clone.w_l, s32[4,2,1,256]{3,2,1,0:T(1,128)} %constant.39.clone.w_r, bf16[64,128]{1,0:T(8,128)(2,1)} %maximum_maximum_fusion.w_t, s32[2,1024,1]{2,1,0:T(8,128)} %constant.40.clone.f_l, s32[2,1,1024]{2,1,0:T(1,128)} %constant.41.clone.f_r, ...), custom_call_target="tpu_custom_call" | custom-call | tf_op jit(solution)/shard_map/chain/pallas_call | solution.py:474
  95.3 2.3 %copy.20 = f32[8,8,4096]{2,1,0:T(8,128)} copy(f32[8,8,4096]{2,1,0:T(8,128)} %bitcast.9) | data formatting | bytes 2097152

commit v4 on v3

--- a/solution.py
+++ b/solution.py
@@ -15,6 +15,7 @@
 LANES = 128
 ROWS = 8
 CHUNKS = 8
+HALVES = 2
 BF = jnp.bfloat16
 F32 = jnp.float32
 VM = 60 * 1024 * 1024
@@ -380,26 +381,36 @@
                 arrived(src_y, c)
             raw[c].wait_send()
 
-    range_kernel(
-        n3, recv2, wide_f, wide_i, spread.at[pl.ds(0, 2)], inf, ini, spread.at[pl.ds(2, 2)], send3
-    )
-    third = []
-    for k in range(1, n3):
-        to = lax.rem(me3 + k, n3)
-        third.append(push(send3.at[to], recv3.at[me3], s3, r3, k, xy(to)))
-    recv3[me3] = send3[me3]
-    for copy in third:
-        copy.wait_recv()
-
-    cfar_kernel(wide_d, recv3, win, send4)
-    fourth = []
-    for k in range(1, xs):
-        to = lax.rem(x + k, xs)
-        fourth.append(push(send4.at[to], recv4.at[x], s4, r4, k, {"pulse": to}))
-    recv4[x] = send4[x]
-    for copy in fourth:
-        copy.wait_recv()
-    place_kernel(recv4, out)
+    third, fourth = [], []
+    part_rows = send3.shape[2]
+    for h in range(HALVES):
+        range_kernel(
+            n3, recv2.at[:, pl.ds(part_rows * h, part_rows)], wide_f, wide_i,
+            spread.at[pl.ds(0, 2)], inf, ini, spread.at[pl.ds(2, 2)], send3.at[h],
+        )
+        for k in range(1, n3):
+            to = lax.rem(me3 + k, n3)
+            third.append(
+                push(send3.at[h, to], recv3.at[h, me3], s3, r3, h * n3 + k, xy(to))
+            )
+        recv3[h, me3] = send3[h, me3]
+
+    for h in range(HALVES):
+        for copy in third[h * (n3 - 1) : (h + 1) * (n3 - 1)]:
+            copy.wait_recv()
+        cfar_kernel(wide_d, recv3.at[h], win, send4.at[h])
+        for k in range(1, xs):
+            to = lax.rem(x + k, xs)
+            fourth.append(
+                push(send4.at[h, to], recv4.at[h, x], s4, r4, h * xs + k, {"pulse": to})
+            )
+        recv4[h, x] = send4[h, x]
+
+    out_rows = send4.shape[2]
+    for h in range(HALVES):
+        for copy in fourth[h * (xs - 1) : (h + 1) * (xs - 1)]:
+            copy.wait_recv()
+        place_kernel(recv4.at[h], out.at[pl.ds(out_rows * h, out_rows)])
     for copy in third + fourth:
         copy.wait_send()
 
@@ -459,8 +470,8 @@
     window = jnp.asarray(((gap > GUARD) & (gap <= GUARD + TRAIN)) / (2.0 * TRAIN), BF)
     dr, di = doppler_table(pulses)
     table = jnp.concatenate([jnp.concatenate([dr, -di], 1), jnp.concatenate([di, dr], 1)], 0)
-    oc, oq, ob, of = grid_ids(2, xs, beam_own, pulse_own)
-    sy, sx, gr, cp, it = grid_ids(ys, xs, groups, 2, ROWS)
+    oc, oq, ob, of = grid_ids(2, xs, beam_own // HALVES, pulse_own)
+    sy, sx, gr, cp, it = grid_ids(ys, xs, groups // HALVES, 2, ROWS)
     bp = gr * ROWS + it
     pulse = sx * pulse_own + sy * part + bp % part
     d_l = ids_pair(oc * pulses + oq * pulse_own + of, ob)[:, :, None]
@@ -483,22 +494,22 @@
             pltpu.VMEM((chunks, kernel_rows // 2, block), BF),
             pltpu.VMEM((chunks, ys, 2, rows, block), BF),
             pltpu.VMEM((ys * chunks, rows, block), BF),
-            pltpu.VMEM((blocks, rows, padded), BF),
-            pltpu.VMEM((blocks, rows, padded), BF),
-            pltpu.VMEM((xs, cells, own), BF),
-            pltpu.VMEM((xs, cells, own), BF),
+            pltpu.VMEM((HALVES, blocks, rows // HALVES, padded), BF),
+            pltpu.VMEM((HALVES, blocks, rows // HALVES, padded), BF),
+            pltpu.VMEM((HALVES, xs, cells // HALVES, own), BF),
+            pltpu.VMEM((HALVES, xs, cells // HALVES, own), BF),
             pltpu.VMEM((2, kernel_rows, depth), BF),
             pltpu.VMEM((m_count * 16, m_count * 16), BF),
             pltpu.VMEM((m_count * 16, m_count * 16), BF),
-            pltpu.VMEM((2 * pulses * beam_own, blocks * rows), BF),
+            pltpu.VMEM((2 * pulses * beam_own // HALVES, blocks * rows // HALVES), BF),
             pltpu.VMEM((4, m_count, ROWS, LANES), F32),
             pltpu.VMEM((chunks, kernel_rows // 2, block), F32),
             dma((chunks,)),
             dma((chunks,)), dma((chunks,)),
             dma((chunks,)), dma((chunks,)),
             dma(((2 * ys - 1) * chunks,)), dma((ys * chunks,)),
-            dma((blocks,)), dma((blocks,)),
-            dma((xs,)), dma((xs,)),
+            dma((HALVES * blocks,)), dma((HALVES * blocks,)),
+            dma((HALVES * xs,)), dma((HALVES * xs,)),
         ],
         compiler_params=pltpu.CompilerParams(
             collective_id=0, has_side_effects=True, vmem_limit_bytes=VM

time: 99.1 us -> 97.8 us (0.987)
  no operation moved by 1% of the time
where the time goes in v4:
time: 97.8 us; the launch traced here: 97 us
  Pallas kernels  90.9 us (93%)
  local copies, waits for them, and re-layouts  3.84 us (4%)
  other arithmetic  2.25 us (2%)
    pallas_call x1, Pallas kernels, shards_chain(): pl.pallas_call(functools.partial(chain_kernel, (zs, ys, xs)), out_shape=j...  90.9 us
    unnamed x1, local copies, waits for them, and re-layouts  2.27 us

profile of v4, /device:TPU:0, one launch (start us, length us, event | category | flops | bytes accessed | tf_op | source)
XLA Modules:
  0.0 97.0 jit_solution(16852997628199885269)
XLA Ops:
  0.0 0.7 fusion
  0.7 0.7 slice_bitcast_fusion
  1.4 0.7 maximum_maximum_fusion.w_t
  2.1 0.9 broadcast_multiply_fusion
  3.0 0.1 mul.12
  3.1 0.7 copy.18
  3.8 90.9 %chain.1 = f32[64,4096]{1,0:T(8,128)} custom-call(bf16[256,4096]{1,0:T(8,128)(2,1)} %bitcast.10, s32[2,512,1]{2,1,0:T(8,128)} %constant.38.clone.w_l, s32[4,2,1,256]{3,2,1,0:T(1,128)} %constant.39.clone.w_r, bf16[64,128]{1,0:T(8,128)(2,1)} %maximum_maximum_fusion.w_t, s32[2,1024,1]{2,1,0:T(8,128)} %constant.40.clone.f_l, s32[2,1,1024]{2,1,0:T(1,128)} %constant.41.clone.f_r, ...), custom_call_target="tpu_custom_call" | custom-call | tf_op jit(solution)/shard_map/chain/pallas_call | solution.py:485
  94.7 2.3 %copy.20 = f32[8,8,4096]{2,1,0:T(8,128)} copy(f32[8,8,4096]{2,1,0:T(8,128)} %bitcast.9) | data formatting | bytes 2097152
